TPU v7x, 16 devices: a whole 2x2x2 slice. The times are simulated.
16 devices in a mesh: dp: 16 (over z, y, x, core).
Axes of the slice: x: 2, y: 2, z: 2, core: 2. Of those that a mesh axis runs over, the one named last changes fastest.
Arguments:
- grad_local: float32 [16, 2500608], P('dp')
- params: float32 [2500608], P('dp')
- accumulator: float32 [2500608], P('dp')
- learn_rate: float32 [], replicated
- clip_max: float32 [], replicated
Outputs:
- output 1: float32 [2500608], P('dp')
- output 2: float32 [2500608], P('dp')
- output 3: bfloat16 [2500608], replicated
- output 4: float32 [], replicated
All inputs are finite; a program needn't handle non-finite values.
Results may differ from a plain program's by a relative error of at most 0.001.
Values sent between devices are 32-bit elements.
A program may use at most 1 GiB of HBM per device.

v0:
```python
import jax
import jax.numpy as jnp
from jax import lax
from jax.sharding import PartitionSpec as P, NamedSharding

EPS = 1e-10


def solution(mesh):
    groups = mesh.shape["dp"]

    def local_step(grad_row, param_blk, accum_blk, learn_rate, clip_max):
        grad_blk = lax.psum_scatter(grad_row[0], "dp", scatter_dimension=0, tiled=True) / groups
        part_sq = jnp.sum(grad_blk * grad_blk)
        grad_norm = jnp.sqrt(lax.psum(part_sq, "dp"))
        clip_scale = jnp.minimum(1.0, clip_max / grad_norm)
        clipped = grad_blk * clip_scale
        accum_new = accum_blk + clipped * clipped
        param_new = param_blk - learn_rate * clipped / (jnp.sqrt(accum_new) + EPS)
        param_full = lax.all_gather(param_new, "dp", axis=0, tiled=True)
        param_copy = lax.optimization_barrier(param_full).astype(jnp.bfloat16)
        return param_new, accum_new, param_copy, grad_norm

    return jax.shard_map(local_step, mesh=mesh, in_specs=(P("dp", None), P("dp"), P("dp"), P(), P()), out_specs=(P("dp"), P("dp"), P(), P()), check_vma=False)
```

profile of v0, /device:TPU:0, one launch (start us, length us, event | category | flops | bytes accessed | tf_op | source)
XLA Modules:
  0.0 252.1 jit_solution(15246352414306392272)
XLA Ops:
  7.2 0.0 copy-start.1
  7.2 0.0 copy-start.2
  7.2 0.0 all-reduce.3.cloned.1.call-start
  7.2 0.7 all-reduce.3.cloned.1.call-update
  7.9 0.0 all-gather.3.cloned.1.call-start
  8.6 132.3 %all-reduce.3.cloned.1.call-done = f32[2500608]{0:T(1024)} async-done(((f32[2500608]{0:T(1024)}), f32[2500608]{0:T(1024)}) %all-reduce.3.cloned.1.call-update) | async-done | bytes 10002448
  141.0 1.9 multiply_reduce_fusion
  143.5 32.1 %psum.7 = f32[]{:T(128)} all-reduce(f32[]{:T(128)} %multiply_reduce_fusion), channel_id=1, replica_groups=mesh['dp'=16] {'dp'}, use_global_device_ids=true, to_apply=%region_2.0 | all-reduce | flops 1 | bytes 8 | tf_op jit(solution)/shard_map/psum | solution.py:15
  176.4 0.0 copy-done.1
  176.4 0.0 copy-done.2
  176.4 2.3 divide_subtract_fusion
  178.7 0.0 copy-start
  178.7 3.6 %reshape.8 = f32[1,1,156288]{2,1,0:T(1,128)} reshape(f32[156288]{0:T(1024)S(1)} %get-tuple-element.4) | data formatting | bytes 1250304
  182.3 0.0 all-gather.3.cloned.1.call-update
  182.4 54.9 %all-gather.3.cloned.1.call-done = f32[16,1,156288]{2,1,0:T(1,128)} async-done(((f32[1,1,156288]{2,1,0:T(1,128)}), f32[16,1,156288]{2,1,0:T(1,128)}) %all-gather.3.cloned.1.call-update) | async-done | bytes 10002448 | tf_op jit(solution)/shard_map/all_gather | solution.py:20
  237.3 6.8 %convert_element_type.3 = bf16[2500608]{0:T(1024)(128)(2,1)} convert(f32[2500608]{0:T(1024)} %bitcast.2) | non-fusion elementwise | flops 2500608 | bytes 15003648 | tf_op jit(solution)/shard_map/convert_element_type | solution.py:21
  244.1 0.0 copy-done
Async XLA Ops:
  7.2 169.2 %copy-start.1 = (f32[156288]{0:T(1024)S(1)}, f32[156288]{0:T(1024)}, u32[]{:S(2)}) copy-start(f32[156288]{0:T(1024)} %param.6) | copy-start | bytes 1875460
  7.2 169.2 %copy-start.2 = (f32[156288]{0:T(1024)S(1)}, f32[156288]{0:T(1024)}, u32[]{:S(2)}) copy-start(f32[156288]{0:T(1024)} %param.7) | copy-start | bytes 1875460
  7.2 133.8 %all-reduce.3.cloned.1.call-start = ((), (), s32[]{:S(2)}) async-start(), calls=%async_computation.1 | async-start | bytes 20004864
  7.9 229.4 %all-gather.3.cloned.1.call-start = ((), (), s32[]{:S(2)}) async-start(), calls=%async_computation | async-start | bytes 10627584 | tf_op jit(solution)/shard_map/all_gather | solution.py:20
  178.7 65.4 %copy-start = (f32[156288]{0:T(1024)}, f32[156288]{0:T(1024)S(1)}, u32[]{:S(2)}) copy-start(f32[156288]{0:T(1024)S(1)} %get-tuple-element.4) | copy-start | bytes 1875460
Sparse Core Ops, SparseCore 0:
  13.2 127.7 all-reduce.2
  182.5 54.7 all-gather.2
where the time goes:
time: 252 us
  waiting for transfers between devices  188 us (75%)
  blocking collectives  32.1 us (13%)
  between operations  17.2 us (7%)
  other arithmetic  11.1 us (4%)
  local copies, waits for them, and re-layouts  3.64 us (1%)
    unnamed x3, waiting for transfers between devices  133 us
    all_gather x1, waiting for transfers between devices, local_step(): param_full = lax.all_gather(param_new, 'dp', axis=0, tiled=True)  54.9 us
    psum x1, blocking collectives, local_step(): grad_norm = jnp.sqrt(lax.psum(part_sq, 'dp'))  32.1 us
    convert_element_type x1, other arithmetic, local_step(): param_copy = lax.optimization_barrier(param_full).astype(jnp.bfloat16)  6.81 us
  transfers between devices with their start and end apart: 2, of which 2 were waited for; matrix products, arithmetic and copies ran while one was open for 0% of the time, Pallas kernels for 0%

commit v1 on v0

v1 whole, which is shorter than its diff:
```python
import functools
import jax
import jax.numpy as jnp
from jax import lax
from jax.sharding import PartitionSpec as P
from jax.experimental import pallas as pl
from jax.experimental.pallas import tpu as pltpu

EPS = 1e-10
LANES = 128
X, Y, Z = 1, 2, 4
ORDERS = ((X, Y, Z), (Y, Z, X), (Z, X, Y))
MESH = pl.DeviceIdType.MESH


def kernel(
    blk, thr, groups,
    rate_ref, clip_ref, grad_hbm, par_hbm, acc_hbm,
    newp_ref, newa_ref, copy_ref, norm_ref,
    own, part, recv, full, par, acc, slots,
    load_sem, pa_sem, d2d_send, d2d_recv, rs_send, rs_recv,
    nrm_send, nrm_recv, ag_send, ag_recv, fwd_send, fwd_recv,
):
    me = lax.axis_index("dp")
    core = me % 2
    chip = me // 2
    x, y, z = chip % 2, (chip // 2) % 2, chip // 4
    partner = me + 1 - 2 * core
    across = {X: me + 2 - 4 * x, Y: me + 4 - 8 * y, Z: me + 8 - 16 * z}

    def base(m, c):
        xc = 1 - x if m & X else x
        yc = 1 - y if m & Y else y
        zc = 1 - z if m & Z else z
        return blk * (2 * (4 * zc + 2 * yc + xc) + c)

    def rows(m, t, c):
        return pl.ds(base(m, c) + thr * t, thr)

    unit = pl.ds(0, thr)

    def remote(src, dst, send, rcv, dev):
        return pltpu.make_async_remote_copy(
            src_ref=src, dst_ref=dst, send_sem=send, recv_sem=rcv,
            device_id=(dev,), device_id_type=MESH)

    order = []
    for pick in (
        lambda a, b, c: a + b + c, lambda a, b, c: a + b, lambda a, b, c: a + c, lambda a, b, c: a,
        lambda a, b, c: b + c, lambda a, b, c: b, lambda a, b, c: c, lambda a, b, c: 0,
    ):
        for t, dims in enumerate(ORDERS):
            order.append((pick(*dims), t))

    loads = {}
    for m, t in order:
        cp = pltpu.make_async_copy(
            grad_hbm.at[rows(m, t, core)], own.at[m, t, unit], load_sem.at[m, t])
        cp.start()
        loads[m, t] = cp
    par_cp = pltpu.make_async_copy(par_hbm, par, pa_sem.at[0])
    par_cp.start()
    acc_cp = pltpu.make_async_copy(acc_hbm, acc, pa_sem.at[1])
    acc_cp.start()

    barrier = pltpu.get_barrier_semaphore()
    for d in range(1, groups):
        pl.semaphore_signal(barrier, inc=1, device_id=((me + d) % groups,), device_id_type=MESH)
    pl.semaphore_wait(barrier, groups - 1)

    d2d = {}
    for m, t in order:
        cp = remote(grad_hbm.at[rows(m, t, 1 - core)], part.at[m, t, unit],
                    d2d_send, d2d_recv.at[m, t], partner)
        cp.start()
        d2d[m, t] = cp

    rs = {}
    slot = {}

    def rs_send_unit(m, t, phase):
        dim = ORDERS[t][phase]
        key = (m ^ dim, t, phase)
        i = slot.setdefault(key, len(slot))
        cp = remote(own.at[m, t, unit], recv.at[i, unit], rs_send, rs_recv.at[i], across[dim])
        cp.start()
        rs[key] = cp

    def rs_add(m, t, phase):
        key = (m, t, phase)
        rs[key].wait_recv()
        own[m, t, unit] = own[m, t, unit] + recv[slot[key], unit]

    for m, t in order:
        loads[m, t].wait()
        d2d[m, t].wait_recv()
        own[m, t, unit] = own[m, t, unit] + part[m, t, unit]
        if m & ORDERS[t][0]:
            rs_send_unit(m, t, 0)

    for step in range(4):
        for t, (a, b, c) in enumerate(ORDERS):
            m = (b + c, b, c, 0)[step]
            rs_add(m, t, 0)
            if m & b:
                rs_send_unit(m, t, 1)
    for step in range(2):
        for t, (a, b, c) in enumerate(ORDERS):
            m = (c, 0)[step]
            rs_add(m, t, 1)
            if m & c:
                rs_send_unit(m, t, 2)
    total = jnp.zeros((1, LANES), jnp.float32)
    for t in range(3):
        rs_add(0, t, 2)
        g = own[0, t, unit] * (1.0 / groups)
        total = total + jnp.sum(g * g, axis=0, keepdims=True)

    slots[pl.ds(me, 1)] = total
    mine = slots.at[pl.ds(me, 1)]
    for d in range(1, groups):
        remote(mine, mine, nrm_send, nrm_recv, (me + d) % groups).start()

    def wait_rows(sem, n):
        ref = full.at[pl.ds(0, n)]
        pltpu.make_async_copy(ref, ref, sem).wait()

    par_cp.wait()
    acc_cp.wait()
    wait_rows(nrm_recv, groups - 1)
    norm = jnp.sqrt(jnp.sum(slots[...]))
    norm_ref[0, 0] = norm
    scale = jnp.minimum(1.0, clip_ref[0, 0] / norm)
    rate = rate_ref[0, 0]

    ag = {}
    fwd = {}

    def ag_send_unit(m, t, phase):
        dim = ORDERS[t][2 - phase]
        r = full.at[rows(m, t, core)]
        cp = remote(r, r, ag_send, ag_recv.at[len(ag)], across[dim])
        cp.start()
        ag[m ^ dim, t] = cp

    def fwd_unit(m, t):
        r = full.at[rows(m, t, core)]
        cp = remote(r, r, fwd_send, fwd_recv.at[m, t], partner)
        cp.start()
        fwd[m, t] = cp

    for t in range(3):
        r = pl.ds(thr * t, thr)
        h = own[0, t, unit] * (1.0 / groups) * scale
        a_new = acc[r] + h * h
        newa_ref[r] = a_new
        w_new = par[r] - rate * h / (jnp.sqrt(a_new) + EPS)
        newp_ref[r] = w_new
        full[rows(0, t, core)] = w_new
        ag_send_unit(0, t, 0)
    for t in range(3):
        ag_send_unit(0, t, 1)
    for t in range(3):
        ag_send_unit(0, t, 2)
    for t in range(3):
        fwd_unit(0, t)

    def arrive(m, t):
        ag[m, t].wait_recv()

    for t, (c, b, a) in enumerate(ORDERS):
        arrive(a, t)
        ag_send_unit(a, t, 1)
        ag_send_unit(a, t, 2)
        fwd_unit(a, t)
    for k in range(2):
        for t, (c, b, a) in enumerate(ORDERS):
            m = (b, b + a)[k]
            arrive(m, t)
            ag_send_unit(m, t, 2)
            fwd_unit(m, t)
    for k in range(4):
        for t, (c, b, a) in enumerate(ORDERS):
            m = (c, c + a, c + b, c + b + a)[k]
            arrive(m, t)
            fwd_unit(m, t)

    for key in fwd:
        fwd[key].wait_recv()
    copy_ref[...] = full[...].astype(jnp.bfloat16)

    wait_rows(d2d_send, 24 * thr)
    wait_rows(rs_send, 21 * thr)
    wait_rows(nrm_send, groups - 1)
    wait_rows(ag_send, 21 * thr)
    wait_rows(fwd_send, 24 * thr)


def solution(mesh):
    groups = mesh.shape["dp"]

    def local_step(grad_row, param_blk, accum_blk, learn_rate, clip_max):
        n = grad_row.shape[1] // LANES
        blk = n // groups
        thr = blk // 3
        pad = -(-thr // 8) * 8
        f32 = jnp.float32
        vm = pl.BlockSpec(memory_space=pltpu.VMEM)
        sm = pl.BlockSpec(memory_space=pltpu.SMEM)
        hb = pl.BlockSpec(memory_space=pl.ANY)
        dma = pltpu.SemaphoreType.DMA
        newp, newa, copy, norm = pl.pallas_call(
            functools.partial(kernel, blk, thr, groups),
            out_shape=(
                jax.ShapeDtypeStruct((blk, LANES), f32),
                jax.ShapeDtypeStruct((blk, LANES), f32),
                jax.ShapeDtypeStruct((n, LANES), jnp.bfloat16),
                jax.ShapeDtypeStruct((1, 1), f32),
            ),
            in_specs=[sm, sm, hb, hb, hb],
            out_specs=(vm, vm, vm, sm),
            scratch_shapes=[
                pltpu.VMEM((8, 3, pad, LANES), f32),
                pltpu.VMEM((8, 3, pad, LANES), f32),
                pltpu.VMEM((21, pad, LANES), f32),
                pltpu.VMEM((n, LANES), f32),
                pltpu.VMEM((blk, LANES), f32),
                pltpu.VMEM((blk, LANES), f32),
                pltpu.VMEM((groups, LANES), f32),
                dma((8, 3)), dma((2,)),
                dma, dma((8, 3)), dma, dma((21,)),
                dma, dma, dma, dma((21,)), dma, dma((8, 3)),
            ],
            compiler_params=pltpu.CompilerParams(
                collective_id=0, has_side_effects=True, vmem_limit_bytes=60 * 1024 * 1024),
        )(learn_rate.reshape(1, 1), clip_max.reshape(1, 1), grad_row.reshape(n, LANES),
          param_blk.reshape(blk, LANES), accum_blk.reshape(blk, LANES))
        return newp.reshape(-1), newa.reshape(-1), copy.reshape(-1), norm.reshape(())

    return jax.shard_map(local_step, mesh=mesh, in_specs=(P("dp", None), P("dp"), P("dp"), P(), P()), out_specs=(P("dp"), P("dp"), P(), P()), check_vma=False)
```

time: 252 us -> 96.1 us (0.38)
  waiting for transfers between devices: 188 us -> 0 us
  Pallas kernels: 0 us -> 82.6 us
  blocking collectives: 32.1 us -> 0 us
  between operations: 17.2 us -> 3.7 us
  other arithmetic: 11.1 us -> 0 us
  local copies, waits for them, and re-layouts: 3.64 us -> 9.46 us
    unnamed x3 -> x0, waiting for transfers between devices: 133 us -> none
    pallas_call x0 -> x1, Pallas kernels: none -> 82.6 us  [local_step(): pl.pallas_call(functools.partial(kernel, blk, thr, groups), out_shape=(ja...]
    all_gather x1 -> x0, waiting for transfers between devices: 54.9 us -> none  [local_step(): param_full = lax.all_gather(param_new, 'dp', axis=0, tiled=True)]
    psum x1 -> x0, blocking collectives: 32.1 us -> none  [local_step(): grad_norm = jnp.sqrt(lax.psum(part_sq, 'dp'))]
    convert_element_type x1 -> x0, other arithmetic: 6.81 us -> none  [local_step(): param_copy = lax.optimization_barrier(param_full).astype(jnp.bfloat16)]
    unnamed x7 -> x3, local copies, waits for them, and re-layouts: 3.64 us -> 9.46 us
  transfers between devices with their start and end apart: 2 -> 0, of which waited for: 2 -> 0; matrix products, arithmetic and copies ran while one was open for 0% -> 0% of each run, Pallas kernels for 0% -> 0%
where the time goes in v1:
time: 96.1 us; the launch traced here: 95.7 us
  Pallas kernels  82.6 us (86%)
  local copies, waits for them, and re-layouts  9.46 us (10%)
  between operations  3.7 us (4%)
    pallas_call x1, Pallas kernels, local_step(): pl.pallas_call(functools.partial(kernel, blk, thr, groups), out_shape=(ja...  82.6 us
    unnamed x3, local copies, waits for them, and re-layouts  9.46 us

profile of v1, /device:TPU:0, one launch (start us, length us, event | category | flops | bytes accessed | tf_op | source)
XLA Modules:
  0.0 95.7 jit_solution(13844546928737211661)
XLA Ops:
  1.9 82.6 %shard_map.84 = (f32[1221,128]{1,0:T(8,128)}, f32[1221,128]{1,0:T(8,128)}, bf16[19536,128]{1,0:T(8,128)(2,1)}, f32[1,1]{1,0:T(1,128)}) custom-call(f32[1,1]{1,0:T(1,128)} %bitcast.9.rate_ref, f32[1,1]{1,0:T(1,128)} %bitcast.10.clip_ref, f32[19536,128]{1,0:T(8,128)} %bitcast.11, f32[1221,128]{1,0:T(8,128)} %bitcast.15, f32[1221,128]{1,0:T(8,128)} %bitcast.16), custom_call_target="tpu_custom_call" | custom-call | tf_op jit(solution)/shard_map/pallas_call | solution.py:212
  84.5 1.9 %copy.15 = f32[156288]{0:T(1024)} copy(f32[156288]{0:T(1024)} %bitcast.14) | data formatting | bytes 1250304
  86.5 1.9 %copy.16 = f32[156288]{0:T(1024)} copy(f32[156288]{0:T(1024)} %bitcast.13) | data formatting | bytes 1250304
  88.4 5.6 %copy.17 = bf16[2500608]{0:T(1024)(128)(2,1)} copy(bf16[2500608]{0:T(1024)(128)(2,1)} %bitcast.12) | data formatting | bytes 10002432

commit v2 on v1

--- a/solution.py
+++ b/solution.py
@@ -11,13 +11,14 @@
 X, Y, Z = 1, 2, 4
 ORDERS = ((X, Y, Z), (Y, Z, X), (Z, X, Y))
 MESH = pl.DeviceIdType.MESH
+TILES = 12
 
 
 def kernel(
     blk, thr, groups,
     rate_ref, clip_ref, grad_hbm, par_hbm, acc_hbm,
-    newp_ref, newa_ref, copy_ref, norm_ref,
-    own, part, recv, full, par, acc, slots,
+    full, newa_ref, norm_ref,
+    own, part, recv, par, acc, slots,
     load_sem, pa_sem, d2d_send, d2d_recv, rs_send, rs_recv,
     nrm_send, nrm_recv, ag_send, ag_recv, fwd_send, fwd_recv,
 ):
@@ -129,9 +130,9 @@
     acc_cp.wait()
     wait_rows(nrm_recv, groups - 1)
     norm = jnp.sqrt(jnp.sum(slots[...]))
-    norm_ref[0, 0] = norm
-    scale = jnp.minimum(1.0, clip_ref[0, 0] / norm)
-    rate = rate_ref[0, 0]
+    norm_ref[...] = jnp.full((1, LANES), norm)
+    scale = jnp.minimum(1.0, clip_ref[...] / norm)
+    rate = rate_ref[...]
 
     ag = {}
     fwd = {}
@@ -155,7 +156,6 @@
         a_new = acc[r] + h * h
         newa_ref[r] = a_new
         w_new = par[r] - rate * h / (jnp.sqrt(a_new) + EPS)
-        newp_ref[r] = w_new
         full[rows(0, t, core)] = w_new
         ag_send_unit(0, t, 0)
     for t in range(3):
@@ -187,13 +187,38 @@
 
     for key in fwd:
         fwd[key].wait_recv()
-    copy_ref[...] = full[...].astype(jnp.bfloat16)
 
     wait_rows(d2d_send, 24 * thr)
     wait_rows(rs_send, 21 * thr)
     wait_rows(nrm_send, groups - 1)
     wait_rows(ag_send, 21 * thr)
     wait_rows(fwd_send, 24 * thr)
+
+
+def write_kernel(blk, tiles, full, newa, norm, newp_hbm, newa_hbm, copy_hbm, norm_ref, buf, sems, copy_sem):
+    me = lax.axis_index("dp")
+    mine = full.at[pl.ds(me * blk, blk)]
+    out = [
+        pltpu.make_async_copy(mine, newp_hbm, sems.at[0]),
+        pltpu.make_async_copy(newa, newa_hbm, sems.at[1]),
+    ]
+    for cp in out:
+        cp.start()
+    n = full.shape[0]
+    edges = [n * i // tiles // 16 * 16 for i in range(tiles)] + [n]
+    for i in range(tiles):
+        r = pl.ds(edges[i], edges[i + 1] - edges[i])
+        buf[r] = full[r].astype(jnp.bfloat16)
+        cp = pltpu.make_async_copy(buf.at[r], copy_hbm.at[r], copy_sem.at[i])
+        cp.start()
+        out.append(cp)
+    norm_ref[...] = norm[:, :1]
+    for cp in out:
+        cp.wait()
+
+
+def in_hbm(a):
+    return pltpu.with_memory_space_constraint(a, pltpu.HBM)
 
 
 def solution(mesh):
@@ -207,23 +232,21 @@
         f32 = jnp.float32
         vm = pl.BlockSpec(memory_space=pltpu.VMEM)
         sm = pl.BlockSpec(memory_space=pltpu.SMEM)
-        hb = pl.BlockSpec(memory_space=pl.ANY)
+        hb = pl.BlockSpec(memory_space=pltpu.HBM)
         dma = pltpu.SemaphoreType.DMA
-        newp, newa, copy, norm = pl.pallas_call(
+        full, newa, norm = pl.pallas_call(
             functools.partial(kernel, blk, thr, groups),
             out_shape=(
-                jax.ShapeDtypeStruct((blk, LANES), f32),
-                jax.ShapeDtypeStruct((blk, LANES), f32),
-                jax.ShapeDtypeStruct((n, LANES), jnp.bfloat16),
-                jax.ShapeDtypeStruct((1, 1), f32),
+                pltpu.VMEM((n, LANES), f32),
+                pltpu.VMEM((blk, LANES), f32),
+                pltpu.VMEM((1, LANES), f32),
             ),
             in_specs=[sm, sm, hb, hb, hb],
-            out_specs=(vm, vm, vm, sm),
+            out_specs=(vm, vm, vm),
             scratch_shapes=[
                 pltpu.VMEM((8, 3, pad, LANES), f32),
                 pltpu.VMEM((8, 3, pad, LANES), f32),
                 pltpu.VMEM((21, pad, LANES), f32),
-                pltpu.VMEM((n, LANES), f32),
                 pltpu.VMEM((blk, LANES), f32),
                 pltpu.VMEM((blk, LANES), f32),
                 pltpu.VMEM((groups, LANES), f32),
@@ -232,9 +255,25 @@
                 dma, dma, dma, dma((21,)), dma, dma((8, 3)),
             ],
             compiler_params=pltpu.CompilerParams(
-                collective_id=0, has_side_effects=True, vmem_limit_bytes=60 * 1024 * 1024),
-        )(learn_rate.reshape(1, 1), clip_max.reshape(1, 1), grad_row.reshape(n, LANES),
-          param_blk.reshape(blk, LANES), accum_blk.reshape(blk, LANES))
+                collective_id=0, has_side_effects=True, vmem_limit_bytes=40 * 1024 * 1024),
+        )(learn_rate, clip_max, in_hbm(grad_row.reshape(n, LANES)),
+          in_hbm(param_blk.reshape(blk, LANES)), in_hbm(accum_blk.reshape(blk, LANES)))
+        newp, newa, copy, norm = pl.pallas_call(
+            functools.partial(write_kernel, blk, TILES),
+            out_shape=(
+                jax.ShapeDtypeStruct((blk, LANES), f32),
+                jax.ShapeDtypeStruct((blk, LANES), f32),
+                jax.ShapeDtypeStruct((n, LANES), jnp.bfloat16),
+                jax.ShapeDtypeStruct((1, 1), f32),
+            ),
+            in_specs=[vm, vm, vm],
+            out_specs=(hb, hb, hb, vm),
+            scratch_shapes=[
+                pltpu.VMEM((n, LANES), jnp.bfloat16),
+                dma((2,)), dma((TILES,)),
+            ],
+            compiler_params=pltpu.CompilerParams(vmem_limit_bytes=12 * 1024 * 1024),
+        )(full, newa, norm)
         return newp.reshape(-1), newa.reshape(-1), copy.reshape(-1), norm.reshape(())
 
     return jax.shard_map(local_step, mesh=mesh, in_specs=(P("dp", None), P("dp"), P("dp"), P(), P()), out_specs=(P("dp"), P("dp"), P(), P()), check_vma=False)

time: 96.1 us -> 85.4 us (0.89)
  local copies, waits for them, and re-layouts: 9.46 us -> 0 us
  between operations: 3.7 us -> 1.93 us
    unnamed x3 -> x0, local copies, waits for them, and re-layouts: 9.46 us -> none
    pallas_call x1 -> x2, Pallas kernels: 82.6 us -> 83.3 us  [the longest x1 80 us: local_step(): pl.pallas_call(functools.partial(kernel, blk, thr, groups), out_shape=(pl...]
where the time goes in v2:
time: 85.4 us; the launch traced here: 85.2 us
  Pallas kernels  83.3 us (98%)
  between operations  1.93 us (2%)
    pallas_call x1, Pallas kernels, local_step(): pl.pallas_call(functools.partial(kernel, blk, thr, groups), out_shape=(pl...  80 us
    pallas_call x1, Pallas kernels, local_step(): pl.pallas_call(functools.partial(write_kernel, blk, TILES), out_shape=(ja...  3.31 us

profile of v2, /device:TPU:0, one launch (start us, length us, event | category | flops | bytes accessed | tf_op | source)
XLA Modules:
  0.0 85.2 jit_solution(5945906586830362441)
XLA Ops:
  1.9 80.0 %shard_map.84 = (f32[19536,128]{1,0:T(8,128)S(1)}, f32[1221,128]{1,0:T(8,128)S(1)}, f32[1,128]{1,0:T(1,128)S(1)}) custom-call(f32[]{:T(128)S(6)} %copy.9.rate_ref, f32[]{:T(128)S(6)} %copy.10.clip_ref, f32[19536,128]{1,0:T(8,128)} %bitcast.7, f32[1221,128]{1,0:T(8,128)} %bitcast.8, f32[1221,128]{1,0:T(8,128)} %bitcast.9), custom_call_target="tpu_custom_call" | custom-call | tf_op jit(solution)/shard_map/pallas_call | solution.py:237
  81.9 3.3 %shard_map.85 = (f32[1221,128]{1,0:T(8,128)}, f32[1221,128]{1,0:T(8,128)}, bf16[19536,128]{1,0:T(8,128)(2,1)}, f32[1,1]{1,0:T(1,128)}) custom-call(f32[19536,128]{1,0:T(8,128)S(1)} %get-tuple-element.11.full, f32[1221,128]{1,0:T(8,128)S(1)} %get-tuple-element.12.newa, f32[1,128]{1,0:T(1,128)S(1)} %get-tuple-element.13.norm), custom_call_target="tpu_custom_call" | custom-call | tf_op jit(solution)/shard_map/pallas_call | solution.py:261

commit v3 on v0

v3 whole, which is shorter than its diff:
```python
import functools
import jax
import jax.numpy as jnp
from jax import lax
from jax.sharding import PartitionSpec as P
from jax.experimental import pallas as pl
from jax.experimental.pallas import tpu as pltpu

EPS = 1e-10
LANES = 128
X, Y, Z = 1, 2, 4
ORDERS = ((X, Y, Z), (Y, Z, X), (Z, X, Y))
MESH = pl.DeviceIdType.MESH
TILES = 12
PIECES = 4


def cut(start, size, n):
    step = -(-size // (8 * n)) * 8
    return [(start + i * step, min(step, size - i * step)) for i in range(n)]


def kernel(
    blk, third, groups,
    rate_ref, clip_ref, grad_hbm, par_hbm, acc_hbm,
    full, newa_ref, norm_ref,
    own, part, recv, par, acc, slots,
    load_sem, near_sem, far_sem, nrm_sem, send_sem,
):
    me = lax.axis_index("dp")
    core = me % 2
    chip = me // 2
    x, y, z = chip % 2, (chip // 2) % 2, chip // 4
    partner = me + 1 - 2 * core
    across = {X: me + 2 - 4 * x, Y: me + 4 - 8 * y, Z: me + 8 - 16 * z}

    def base(m, c):
        xc = 1 - x if m & X else x
        yc = 1 - y if m & Y else y
        zc = 1 - z if m & Z else z
        return blk * (2 * (4 * zc + 2 * yc + xc) + c)

    thirds = [(third * t, min(third, blk - third * t)) for t in range(3)]

    def send(src, dst, kind, rcv, dev):
        pltpu.make_async_remote_copy(
            src_ref=src, dst_ref=dst, send_sem=send_sem.at[kind], recv_sem=rcv,
            device_id=(dev,), device_id_type=MESH).start()

    def wait_rows(sem, n):
        ref = full.at[pl.ds(0, n)]
        pltpu.make_async_copy(ref, ref, sem).wait()

    waves = ((X + Y + Z,), (X + Y, Y + Z, Z + X), (X, Y, Z, 0))
    for i, wave in enumerate(waves):
        for m in wave:
            pltpu.make_async_copy(
                grad_hbm.at[pl.ds(base(m, core), blk)], own.at[m, pl.ds(0, blk)], load_sem.at[i]).start()
    par_cp = pltpu.make_async_copy(par_hbm, par, load_sem.at[3])
    par_cp.start()
    acc_cp = pltpu.make_async_copy(acc_hbm, acc, load_sem.at[4])
    acc_cp.start()

    barrier = pltpu.get_barrier_semaphore()
    near = (partner, across[X], across[Y], across[Z])
    for dev in near:
        pl.semaphore_signal(barrier, inc=1, device_id=(dev,), device_id_type=MESH)
    pl.semaphore_wait(barrier, len(near))

    all_bits = X + Y + Z
    pieces = [cut(*thirds[t], PIECES) for t in range(3)]

    def exchange(m, start, size, i):
        send(grad_hbm.at[pl.ds(base(m, 1 - core) + start, size)],
             part.at[m, pl.ds(start, size)], 0, near_sem.at[i], partner)

    for p in range(PIECES):
        for t in range(3):
            exchange(all_bits, *pieces[t][p], p)
    for i in (1, 2):
        for m in waves[i]:
            exchange(m, 0, blk, PIECES - 1 + i)

    def fold(m, start, size):
        r = pl.ds(start, size)
        own[m, r] = own[m, r] + part[m, r]

    def unit(step, t):
        a, b, c = ORDERS[t]
        return (b + c, b, c, 0, c, 0, 0)[step]

    PHASE = (0, 0, 0, 0, 1, 1, 2)

    def push(step, t, start, size):
        dim = ORDERS[t][PHASE[step]]
        s0 = thirds[t][0]
        send(own.at[unit(step, t) ^ dim, pl.ds(start, size)],
             recv.at[3 * step + t, pl.ds(start - s0, size)], 1, far_sem.at[step], across[dim])

    load_waits = [len(w) * blk for w in waves]
    wait_rows(load_sem.at[0], load_waits[0])
    for p in range(PIECES):
        wait_rows(near_sem.at[p], sum(pieces[t][p][1] for t in range(3)))
        for t in range(3):
            fold(all_bits, *pieces[t][p])
            push(0, t, *pieces[t][p])
    wait_rows(load_sem.at[1], load_waits[1])
    wait_rows(near_sem.at[PIECES], load_waits[1])
    for step in (1, 2):
        for t in range(3):
            fold(unit(step, t) ^ ORDERS[t][0], *thirds[t])
            push(step, t, *thirds[t])
    wait_rows(load_sem.at[2], load_waits[2])
    wait_rows(near_sem.at[PIECES + 1], load_waits[2])
    for t in range(3):
        fold(unit(3, t) ^ ORDERS[t][0], *thirds[t])
        push(3, t, *thirds[t])
    for step in range(4):
        for t in range(3):
            fold(unit(step, t), *thirds[t])

    total = jnp.zeros((1, LANES), jnp.float32)
    for step in range(7):
        wait_rows(far_sem.at[step], blk)
        for t in range(3):
            m = unit(step, t)
            s0, size = thirds[t]
            got = own[m, pl.ds(s0, size)] + recv[3 * step + t, pl.ds(0, size)]
            own[m, pl.ds(s0, size)] = got
            if step in (0, 1):
                push(4 + step, t, *thirds[t])
            if step == 4:
                push(6, t, *thirds[t])
            if step == 6:
                g = got * (1.0 / groups)
                total = total + jnp.sum(g * g, axis=0, keepdims=True)

    slots[pl.ds(me, 1)] = total
    mine = slots.at[pl.ds(me, 1)]
    for d in range(1, groups):
        send(mine, mine, 2, nrm_sem, (me + d) % groups)
    par_cp.wait()
    acc_cp.wait()
    wait_rows(nrm_sem, groups - 1)
    square = jnp.sum(jnp.sum(slots[...], axis=0, keepdims=True), axis=1, keepdims=True)
    norm = jnp.sqrt(square)
    norm_ref[...] = norm
    scale = jnp.minimum(1.0, clip_ref[...] / norm)
    rate = rate_ref[...]

    def rows(m, start, size):
        return full.at[pl.ds(base(m, core) + start, size)]

    def gather(m, t, j, rcv, start, size):
        send(rows(m, start, size), rows(m, start, size), 3, rcv, across[ORDERS[t][2 - j]])

    def forward(m, start, size):
        send(rows(m, start, size), rows(m, start, size), 4, near_sem.at[PIECES], partner)

    for p in range(PIECES):
        for t in range(3):
            start, size = pieces[t][p]
            r = pl.ds(start, size)
            h = own[0, r] * (1.0 / groups) * scale
            a_new = acc[r] + h * h
            newa_ref[r] = a_new
            full[pl.ds(base(0, core) + start, size)] = par[r] - rate * h / (jnp.sqrt(a_new) + EPS)
            gather(0, t, 0, far_sem.at[0], start, size)
    for j in (1, 2):
        for t in range(3):
            gather(0, t, j, far_sem.at[j], *thirds[t])
    forward(0, 0, blk)

    for step in range(6):
        wait_rows(far_sem.at[step], blk)
        for t in range(3):
            c, b, a = ORDERS[t]
            m = (a, b, c, a + b, a + c, b + c)[step]
            if step == 0:
                gather(m, t, 1, far_sem.at[3], *thirds[t])
            if step in (0, 1):
                gather(m, t, 2, far_sem.at[4 + step], *thirds[t])
            if step == 3:
                for p in range(PIECES):
                    gather(m, t, 2, near_sem.at[p], *pieces[t][p])
        for t in range(3):
            c, b, a = ORDERS[t]
            forward((a, b, c, a + b, a + c, b + c)[step], *thirds[t])
    for p in range(PIECES):
        wait_rows(near_sem.at[p], sum(pieces[t][p][1] for t in range(3)))
        for t in range(3):
            forward(all_bits, *pieces[t][p])
    wait_rows(near_sem.at[PIECES], 8 * blk)

    for kind, n in enumerate((8 * blk, 7 * blk, groups - 1, 7 * blk, 8 * blk)):
        wait_rows(send_sem.at[kind], n)


def write_kernel(blk, full, newa, norm, newp_hbm, newa_hbm, copy_hbm, norm_hbm, buf, sems):
    me = lax.axis_index("dp")
    mine = full.at[pl.ds(me * blk, blk)]
    out = [
        pltpu.make_async_copy(mine, newp_hbm, sems.at[0]),
        pltpu.make_async_copy(newa, newa_hbm, sems.at[1]),
        pltpu.make_async_copy(norm, norm_hbm, sems.at[2]),
    ]
    for cp in out:
        cp.start()
    n = full.shape[0]
    edges = [n * i // TILES // 16 * 16 for i in range(TILES)] + [n]
    for i in range(TILES):
        r = pl.ds(edges[i], edges[i + 1] - edges[i])
        buf[r] = full[r].astype(jnp.bfloat16)
        pltpu.make_async_copy(buf.at[r], copy_hbm.at[r], sems.at[3]).start()
    pltpu.make_async_copy(buf, copy_hbm, sems.at[3]).wait()
    for cp in out:
        cp.wait()


def in_hbm(a):
    return pltpu.with_memory_space_constraint(a, pltpu.HBM)


def solution(mesh):
    groups = mesh.shape["dp"]

    def local_step(grad_row, param_blk, accum_blk, learn_rate, clip_max):
        n = grad_row.shape[1] // LANES
        blk = n // groups
        third = -(-blk // 24) * 8
        pad = -(-blk // 8) * 8
        f32 = jnp.float32
        vm = pl.BlockSpec(memory_space=pltpu.VMEM)
        sm = pl.BlockSpec(memory_space=pltpu.SMEM)
        hb = pl.BlockSpec(memory_space=pltpu.HBM)
        dma = pltpu.SemaphoreType.DMA
        full, newa, norm = pl.pallas_call(
            functools.partial(kernel, blk, third, groups),
            out_shape=(
                pltpu.VMEM((n, LANES), f32),
                pltpu.VMEM((blk, LANES), f32),
                pltpu.VMEM((1, 1), f32),
            ),
            in_specs=[sm, sm, hb, hb, hb],
            out_specs=(vm, vm, vm),
            scratch_shapes=[
                pltpu.VMEM((8, pad, LANES), f32),
                pltpu.VMEM((8, pad, LANES), f32),
                pltpu.VMEM((21, third, LANES), f32),
                pltpu.VMEM((blk, LANES), f32),
                pltpu.VMEM((blk, LANES), f32),
                pltpu.VMEM((groups, LANES), f32),
                dma((5,)), dma((PIECES + 2,)), dma((7,)), dma, dma((5,)),
            ],
            compiler_params=pltpu.CompilerParams(
                collective_id=0, has_side_effects=True, vmem_limit_bytes=40 * 1024 * 1024),
        )(learn_rate, clip_max, in_hbm(grad_row.reshape(n, LANES)),
          in_hbm(param_blk.reshape(blk, LANES)), in_hbm(accum_blk.reshape(blk, LANES)))
        newp, newa, copy, norm = pl.pallas_call(
            functools.partial(write_kernel, blk),
            out_shape=(
                jax.ShapeDtypeStruct((blk, LANES), f32),
                jax.ShapeDtypeStruct((blk, LANES), f32),
                jax.ShapeDtypeStruct((n, LANES), jnp.bfloat16),
                jax.ShapeDtypeStruct((1, 1), f32),
            ),
            in_specs=[vm, vm, vm],
            out_specs=(hb, hb, hb, hb),
            scratch_shapes=[pltpu.VMEM((n, LANES), jnp.bfloat16), dma((4,))],
            compiler_params=pltpu.CompilerParams(vmem_limit_bytes=12 * 1024 * 1024),
        )(full, newa, norm)
        return newp.reshape(-1), newa.reshape(-1), copy.reshape(-1), norm.reshape(())

    return jax.shard_map(local_step, mesh=mesh, in_specs=(P("dp", None), P("dp"), P("dp"), P(), P()), out_specs=(P("dp"), P("dp"), P(), P()), check_vma=False)
```

time: 252 us -> 82.4 us (0.33)
  waiting for transfers between devices: 188 us -> 0 us
  Pallas kernels: 0 us -> 80.4 us
  blocking collectives: 32.1 us -> 0 us
  between operations: 17.2 us -> 1.93 us
  other arithmetic: 11.1 us -> 0 us
  local copies, waits for them, and re-layouts: 3.64 us -> 0 us
    unnamed x3 -> x0, waiting for transfers between devices: 133 us -> none
    pallas_call x0 -> x2, Pallas kernels: none -> 80.4 us  [the longest x1 77 us: local_step(): pl.pallas_call(functools.partial(kernel, blk, third, groups), out_shape=(...]
    all_gather x1 -> x0, waiting for transfers between devices: 54.9 us -> none  [local_step(): param_full = lax.all_gather(param_new, 'dp', axis=0, tiled=True)]
    psum x1 -> x0, blocking collectives: 32.1 us -> none  [local_step(): grad_norm = jnp.sqrt(lax.psum(part_sq, 'dp'))]
    convert_element_type x1 -> x0, other arithmetic: 6.81 us -> none  [local_step(): param_copy = lax.optimization_barrier(param_full).astype(jnp.bfloat16)]
    unnamed x7 -> x0, local copies, waits for them, and re-layouts: 3.64 us -> none
  transfers between devices with their start and end apart: 2 -> 0, of which waited for: 2 -> 0; matrix products, arithmetic and copies ran while one was open for 0% -> 0% of each run, Pallas kernels for 0% -> 0%
where the time goes in v3:
time: 82.4 us; the launch traced here: 82.3 us
  Pallas kernels  80.4 us (98%)
  between operations  1.93 us (2%)
    pallas_call x1, Pallas kernels, local_step(): pl.pallas_call(functools.partial(kernel, blk, third, groups), out_shape=(...  77 us
    pallas_call x1, Pallas kernels, local_step(): pl.pallas_call(functools.partial(write_kernel, blk), out_shape=(jax.Shape...  3.32 us

profile of v3, /device:TPU:0, one launch (start us, length us, event | category | flops | bytes accessed | tf_op | source)
XLA Modules:
  0.0 82.3 jit_solution(18108719050964382086)
XLA Ops:
  1.9 77.0 %shard_map.84 = (f32[19536,128]{1,0:T(8,128)S(1)}, f32[1221,128]{1,0:T(8,128)S(1)}, f32[1,1]{1,0:T(1,128)}) custom-call(f32[]{:T(128)S(6)} %copy.9.rate_ref, f32[]{:T(128)S(6)} %copy.10.clip_ref, f32[19536,128]{1,0:T(8,128)} %bitcast.7, f32[1221,128]{1,0:T(8,128)} %bitcast.8, f32[1221,128]{1,0:T(8,128)} %bitcast.9), custom_call_target="tpu_custom_call" | custom-call | tf_op jit(solution)/shard_map/pallas_call | solution.py:237
  79.0 3.3 %shard_map.85 = (f32[1221,128]{1,0:T(8,128)}, f32[1221,128]{1,0:T(8,128)}, bf16[19536,128]{1,0:T(8,128)(2,1)}, f32[1,1]{1,0:T(1,128)}) custom-call(f32[19536,128]{1,0:T(8,128)S(1)} %get-tuple-element.11.full, f32[1221,128]{1,0:T(8,128)S(1)} %get-tuple-element.12.newa, f32[1,1]{1,0:T(1,128)} %get-tuple-element.13.norm), custom_call_target="tpu_custom_call" | custom-call | tf_op jit(solution)/shard_map/pallas_call | solution.py:259

commit v4 on v3

--- a/solution.py
+++ b/solution.py
@@ -34,11 +34,14 @@
     partner = me + 1 - 2 * core
     across = {X: me + 2 - 4 * x, Y: me + 4 - 8 * y, Z: me + 8 - 16 * z}
 
-    def base(m, c):
+    def place(m, c):
         xc = 1 - x if m & X else x
         yc = 1 - y if m & Y else y
         zc = 1 - z if m & Z else z
-        return blk * (2 * (4 * zc + 2 * yc + xc) + c)
+        return 2 * (4 * zc + 2 * yc + xc) + c
+
+    def base(m, c):
+        return blk * place(m, c)
 
     thirds = [(third * t, min(third, blk - third * t)) for t in range(3)]
 
@@ -137,25 +140,27 @@
 
     slots[pl.ds(me, 1)] = total
     mine = slots.at[pl.ds(me, 1)]
-    for d in range(1, groups):
-        send(mine, mine, 2, nrm_sem, (me + d) % groups)
+    for m in (7, 3, 6, 5, 1, 2, 4):
+        for c in (core, 1 - core):
+            send(mine, mine, 2, nrm_sem, place(m, c))
+    send(mine, mine, 2, nrm_sem, partner)
     par_cp.wait()
     acc_cp.wait()
     wait_rows(nrm_sem, groups - 1)
     square = jnp.sum(jnp.sum(slots[...], axis=0, keepdims=True), axis=1, keepdims=True)
     norm = jnp.sqrt(square)
-    norm_ref[...] = norm
+    norm_ref[...] = jnp.broadcast_to(norm, (1, LANES))
     scale = jnp.minimum(1.0, clip_ref[...] / norm)
     rate = rate_ref[...]
 
-    def rows(m, start, size):
-        return full.at[pl.ds(base(m, core) + start, size)]
+    def rows(m, start, size, c=core):
+        return full.at[pl.ds(base(m, c) + start, size)]
 
     def gather(m, t, j, rcv, start, size):
         send(rows(m, start, size), rows(m, start, size), 3, rcv, across[ORDERS[t][2 - j]])
 
-    def forward(m, start, size):
-        send(rows(m, start, size), rows(m, start, size), 4, near_sem.at[PIECES], partner)
+    def forward(m, start, size, c=core):
+        send(rows(m, start, size, c), rows(m, start, size, c), 4, near_sem.at[PIECES], partner)
 
     for p in range(PIECES):
         for t in range(3):
@@ -182,27 +187,29 @@
                 gather(m, t, 2, far_sem.at[4 + step], *thirds[t])
             if step == 3:
                 for p in range(PIECES):
-                    gather(m, t, 2, near_sem.at[p], *pieces[t][p])
+                    r = rows(m, *pieces[t][p])
+                    send(r, r, 3, near_sem.at[p], place(ORDERS[t][0], 1 - core))
         for t in range(3):
             c, b, a = ORDERS[t]
             forward((a, b, c, a + b, a + c, b + c)[step], *thirds[t])
     for p in range(PIECES):
         wait_rows(near_sem.at[p], sum(pieces[t][p][1] for t in range(3)))
         for t in range(3):
-            forward(all_bits, *pieces[t][p])
+            forward(all_bits, *pieces[t][p], 1 - core)
     wait_rows(near_sem.at[PIECES], 8 * blk)
 
     for kind, n in enumerate((8 * blk, 7 * blk, groups - 1, 7 * blk, 8 * blk)):
         wait_rows(send_sem.at[kind], n)
 
 
-def write_kernel(blk, full, newa, norm, newp_hbm, newa_hbm, copy_hbm, norm_hbm, buf, sems):
+def write_kernel(blk, full, newa, norm, newp_hbm, newa_hbm, copy_hbm, norm_hbm, buf, one, sems):
     me = lax.axis_index("dp")
     mine = full.at[pl.ds(me * blk, blk)]
+    one[...] = norm[:, :1]
     out = [
         pltpu.make_async_copy(mine, newp_hbm, sems.at[0]),
         pltpu.make_async_copy(newa, newa_hbm, sems.at[1]),
-        pltpu.make_async_copy(norm, norm_hbm, sems.at[2]),
+        pltpu.make_async_copy(one, norm_hbm, sems.at[2]),
     ]
     for cp in out:
         cp.start()
@@ -239,7 +246,7 @@
             out_shape=(
                 pltpu.VMEM((n, LANES), f32),
                 pltpu.VMEM((blk, LANES), f32),
-                pltpu.VMEM((1, 1), f32),
+                pltpu.VMEM((1, LANES), f32),
             ),
             in_specs=[sm, sm, hb, hb, hb],
             out_specs=(vm, vm, vm),
@@ -266,7 +273,7 @@
             ),
             in_specs=[vm, vm, vm],
             out_specs=(hb, hb, hb, hb),
-            scratch_shapes=[pltpu.VMEM((n, LANES), jnp.bfloat16), dma((4,))],
+            scratch_shapes=[pltpu.VMEM((n, LANES), jnp.bfloat16), pltpu.VMEM((1, 1), f32), dma((4,))],
             compiler_params=pltpu.CompilerParams(vmem_limit_bytes=12 * 1024 * 1024),
         )(full, newa, norm)
         return newp.reshape(-1), newa.reshape(-1), copy.reshape(-1), norm.reshape(())

time: 82.4 us -> 80.9 us (0.982)
  Pallas kernels: 80.4 us -> 78.8 us
    pallas_call x1, Pallas kernels: 77 us -> 76.1 us  [local_step(): pl.pallas_call(functools.partial(kernel, blk, third, groups), out_shape=(...]
where the time goes in v4:
time: 80.9 us; the launch traced here: 80.7 us
  Pallas kernels  78.8 us (97%)
  between operations  1.93 us (2%)
    pallas_call x1, Pallas kernels, local_step(): pl.pallas_call(functools.partial(kernel, blk, third, groups), out_shape=(...  76.1 us
    pallas_call x1, Pallas kernels, local_step(): pl.pallas_call(functools.partial(write_kernel, blk), out_shape=(jax.Shape...  2.69 us

profile of v4, /device:TPU:0, one launch (start us, length us, event | category | flops | bytes accessed | tf_op | source)
XLA Modules:
  0.0 80.7 jit_solution(3431220495160397352)
XLA Ops:
  1.9 76.1 %shard_map.84 = (f32[19536,128]{1,0:T(8,128)S(1)}, f32[1221,128]{1,0:T(8,128)S(1)}, f32[1,128]{1,0:T(1,128)S(1)}) custom-call(f32[]{:T(128)S(6)} %copy.9.rate_ref, f32[]{:T(128)S(6)} %copy.10.clip_ref, f32[19536,128]{1,0:T(8,128)} %bitcast.7, f32[1221,128]{1,0:T(8,128)} %bitcast.8, f32[1221,128]{1,0:T(8,128)} %bitcast.9), custom_call_target="tpu_custom_call" | custom-call | tf_op jit(solution)/shard_map/pallas_call | solution.py:244
  78.1 2.7 %shard_map.85 = (f32[1221,128]{1,0:T(8,128)}, f32[1221,128]{1,0:T(8,128)}, bf16[19536,128]{1,0:T(8,128)(2,1)}, f32[1,1]{1,0:T(1,128)}) custom-call(f32[19536,128]{1,0:T(8,128)S(1)} %get-tuple-element.11.full, f32[1221,128]{1,0:T(8,128)S(1)} %get-tuple-element.12.newa, f32[1,128]{1,0:T(1,128)S(1)} %get-tuple-element.13.norm), custom_call_target="tpu_custom_call" | custom-call | tf_op jit(solution)/shard_map/pallas_call | solution.py:266

commit v5 on v4

--- a/solution.py
+++ b/solution.py
@@ -24,8 +24,8 @@
     blk, third, groups,
     rate_ref, clip_ref, grad_hbm, par_hbm, acc_hbm,
     full, newa_ref, norm_ref,
-    own, part, recv, par, acc, slots,
-    load_sem, near_sem, far_sem, nrm_sem, send_sem,
+    own, part, recv, par, acc, slots, raw,
+    load_sem, near_sem, far_sem, nrm_sem, raw_sem, send_sem,
 ):
     me = lax.axis_index("dp")
     core = me % 2
@@ -122,6 +122,13 @@
         for t in range(3):
             fold(unit(step, t), *thirds[t])
 
+    def early(t, k, src):
+        start, size = pieces[t][0]
+        send(src.at[pl.ds(start, size)], raw.at[3 * t + k, pl.ds(0, size)], 5, raw_sem, across[ORDERS[t][2]])
+
+    n_raw = 3 * sum(pieces[t][0][1] for t in range(3))
+    par_cp.wait()
+    acc_cp.wait()
     total = jnp.zeros((1, LANES), jnp.float32)
     for step in range(7):
         wait_rows(far_sem.at[step], blk)
@@ -137,6 +144,10 @@
             if step == 6:
                 g = got * (1.0 / groups)
                 total = total + jnp.sum(g * g, axis=0, keepdims=True)
+        if step == 4:
+            for t in range(3):
+                early(t, 0, par)
+                early(t, 1, acc)
 
     slots[pl.ds(me, 1)] = total
     mine = slots.at[pl.ds(me, 1)]
@@ -144,8 +155,8 @@
         for c in (core, 1 - core):
             send(mine, mine, 2, nrm_sem, place(m, c))
     send(mine, mine, 2, nrm_sem, partner)
-    par_cp.wait()
-    acc_cp.wait()
+    for t in range(3):
+        early(t, 2, own.at[0])
     wait_rows(nrm_sem, groups - 1)
     square = jnp.sum(jnp.sum(slots[...], axis=0, keepdims=True), axis=1, keepdims=True)
     norm = jnp.sqrt(square)
@@ -162,22 +173,31 @@
     def forward(m, start, size, c=core):
         send(rows(m, start, size, c), rows(m, start, size, c), 4, near_sem.at[PIECES], partner)
 
-    for p in range(PIECES):
+    def update(w, a, total):
+        h = total * (1.0 / groups) * scale
+        a_new = a + h * h
+        return a_new, w - rate * h / (jnp.sqrt(a_new) + EPS)
+
+    for p in (*range(1, PIECES), 0):
         for t in range(3):
             start, size = pieces[t][p]
             r = pl.ds(start, size)
-            h = own[0, r] * (1.0 / groups) * scale
-            a_new = acc[r] + h * h
-            newa_ref[r] = a_new
-            full[pl.ds(base(0, core) + start, size)] = par[r] - rate * h / (jnp.sqrt(a_new) + EPS)
-            gather(0, t, 0, far_sem.at[0], start, size)
+            newa_ref[r], full[pl.ds(base(0, core) + start, size)] = update(par[r], acc[r], own[0, r])
+            if p:
+                gather(0, t, 0, far_sem.at[0], start, size)
     for j in (1, 2):
         for t in range(3):
             gather(0, t, j, far_sem.at[j], *thirds[t])
     forward(0, 0, blk)
+    wait_rows(raw_sem, n_raw)
+    for t in range(3):
+        start, size = pieces[t][0]
+        r = pl.ds(0, size)
+        full[pl.ds(base(ORDERS[t][2], core) + start, size)] = update(
+            raw[3 * t, r], raw[3 * t + 1, r], raw[3 * t + 2, r])[1]
 
     for step in range(6):
-        wait_rows(far_sem.at[step], blk)
+        wait_rows(far_sem.at[step], blk if step else blk - n_raw // 3)
         for t in range(3):
             c, b, a = ORDERS[t]
             m = (a, b, c, a + b, a + c, b + c)[step]
@@ -198,7 +218,7 @@
             forward(all_bits, *pieces[t][p], 1 - core)
     wait_rows(near_sem.at[PIECES], 8 * blk)
 
-    for kind, n in enumerate((8 * blk, 7 * blk, groups - 1, 7 * blk, 8 * blk)):
+    for kind, n in enumerate((8 * blk, 7 * blk, groups - 1, 7 * blk - n_raw // 3, 8 * blk, n_raw)):
         wait_rows(send_sem.at[kind], n)
 
 
@@ -257,7 +277,8 @@
                 pltpu.VMEM((blk, LANES), f32),
                 pltpu.VMEM((blk, LANES), f32),
                 pltpu.VMEM((groups, LANES), f32),
-                dma((5,)), dma((PIECES + 2,)), dma((7,)), dma, dma((5,)),
+                pltpu.VMEM((9, third, LANES), f32),
+                dma((5,)), dma((PIECES + 2,)), dma((7,)), dma, dma, dma((6,)),
             ],
             compiler_params=pltpu.CompilerParams(
                 collective_id=0, has_side_effects=True, vmem_limit_bytes=40 * 1024 * 1024),

time: 80.9 us -> 79.9 us (0.988)
  Pallas kernels: 78.8 us -> 77.9 us
    pallas_call x1, Pallas kernels: 76.1 us -> 75.2 us  [local_step(): pl.pallas_call(functools.partial(kernel, blk, third, groups), out_shape=(...]
where the time goes in v5:
time: 79.9 us; the launch traced here: 79.8 us
  Pallas kernels  77.9 us (97%)
  between operations  1.93 us (2%)
    pallas_call x1, Pallas kernels, local_step(): pl.pallas_call(functools.partial(kernel, blk, third, groups), out_shape=(...  75.2 us
    pallas_call x1, Pallas kernels, local_step(): pl.pallas_call(functools.partial(write_kernel, blk), out_shape=(jax.Shape...  2.69 us

profile of v5, /device:TPU:0, one launch (start us, length us, event | category | flops | bytes accessed | tf_op | source)
XLA Modules:
  0.0 79.8 jit_solution(17470489547096565516)
XLA Ops:
  1.9 75.2 %shard_map.84 = (f32[19536,128]{1,0:T(8,128)S(1)}, f32[1221,128]{1,0:T(8,128)S(1)}, f32[1,128]{1,0:T(1,128)S(1)}) custom-call(f32[]{:T(128)S(6)} %copy.9.rate_ref, f32[]{:T(128)S(6)} %copy.10.clip_ref, f32[19536,128]{1,0:T(8,128)} %bitcast.7, f32[1221,128]{1,0:T(8,128)} %bitcast.8, f32[1221,128]{1,0:T(8,128)} %bitcast.9), custom_call_target="tpu_custom_call" | custom-call | tf_op jit(solution)/shard_map/pallas_call | solution.py:264
  77.1 2.7 %shard_map.85 = (f32[1221,128]{1,0:T(8,128)}, f32[1221,128]{1,0:T(8,128)}, bf16[19536,128]{1,0:T(8,128)(2,1)}, f32[1,1]{1,0:T(1,128)}) custom-call(f32[19536,128]{1,0:T(8,128)S(1)} %get-tuple-element.11.full, f32[1221,128]{1,0:T(8,128)S(1)} %get-tuple-element.12.newa, f32[1,128]{1,0:T(1,128)S(1)} %get-tuple-element.13.norm), custom_call_target="tpu_custom_call" | custom-call | tf_op jit(solution)/shard_map/pallas_call | solution.py:287

commit v6 on v5

--- a/solution.py
+++ b/solution.py
@@ -12,7 +12,11 @@
 ORDERS = ((X, Y, Z), (Y, Z, X), (Z, X, Y))
 MESH = pl.DeviceIdType.MESH
 TILES = 12
-PIECES = 4
+PIECES = 6
+AHEAD = 104
+EARLY = 160
+BOTH = 112
+FIRST = 64
 
 
 def cut(start, size, n):
@@ -24,7 +28,7 @@
     blk, third, groups,
     rate_ref, clip_ref, grad_hbm, par_hbm, acc_hbm,
     full, newa_ref, norm_ref,
-    own, part, recv, par, acc, slots, raw,
+    own, part, recv, other, par, acc, slots, raw,
     load_sem, near_sem, far_sem, nrm_sem, raw_sem, send_sem,
 ):
     me = lax.axis_index("dp")
@@ -65,18 +69,23 @@
     acc_cp.start()
 
     barrier = pltpu.get_barrier_semaphore()
-    near = (partner, across[X], across[Y], across[Z])
+    near = [place(d, c) for d in (X, Y, Z) for c in (core, 1 - core)] + [partner]
     for dev in near:
         pl.semaphore_signal(barrier, inc=1, device_id=(dev,), device_id_type=MESH)
     pl.semaphore_wait(barrier, len(near))
 
     all_bits = X + Y + Z
-    pieces = [cut(*thirds[t], PIECES) for t in range(3)]
+    pieces = [cut(s0 + FIRST, size - FIRST, PIECES) for s0, size in thirds]
 
     def exchange(m, start, size, i):
         send(grad_hbm.at[pl.ds(base(m, 1 - core) + start, size)],
              part.at[m, pl.ds(start, size)], 0, near_sem.at[i], partner)
 
+    for t in range(3):
+        s0, _ = thirds[t]
+        for c, dst in ((core, recv), (1 - core, other)):
+            send(grad_hbm.at[pl.ds(base(all_bits, c) + s0, FIRST)], dst.at[t, pl.ds(0, FIRST)],
+                 1, far_sem.at[0], place(ORDERS[t][0], c))
     for p in range(PIECES):
         for t in range(3):
             exchange(all_bits, *pieces[t][p], p)
@@ -122,19 +131,22 @@
         for t in range(3):
             fold(unit(step, t), *thirds[t])
 
-    def early(t, k, src):
-        start, size = pieces[t][0]
-        send(src.at[pl.ds(start, size)], raw.at[3 * t + k, pl.ds(0, size)], 5, raw_sem, across[ORDERS[t][2]])
-
-    n_raw = 3 * sum(pieces[t][0][1] for t in range(3))
+    def early(k, src, lo, hi):
+        for t in range(3):
+            send(src.at[pl.ds(thirds[t][0] + lo, hi - lo)], raw.at[3 * t + k, pl.ds(lo, hi - lo)],
+                 5, raw_sem, across[ORDERS[t][2]])
+
     par_cp.wait()
     acc_cp.wait()
     total = jnp.zeros((1, LANES), jnp.float32)
     for step in range(7):
-        wait_rows(far_sem.at[step], blk)
+        wait_rows(far_sem.at[step], blk if step else blk + 3 * FIRST)
         for t in range(3):
             m = unit(step, t)
             s0, size = thirds[t]
+            if step == 0:
+                r = pl.ds(0, FIRST)
+                recv[t, r] = recv[t, r] + other[t, r]
             got = own[m, pl.ds(s0, size)] + recv[3 * step + t, pl.ds(0, size)]
             own[m, pl.ds(s0, size)] = got
             if step in (0, 1):
@@ -145,9 +157,8 @@
                 g = got * (1.0 / groups)
                 total = total + jnp.sum(g * g, axis=0, keepdims=True)
         if step == 4:
-            for t in range(3):
-                early(t, 0, par)
-                early(t, 1, acc)
+            early(0, par, 0, AHEAD)
+            early(1, acc, 0, AHEAD)
 
     slots[pl.ds(me, 1)] = total
     mine = slots.at[pl.ds(me, 1)]
@@ -155,8 +166,9 @@
         for c in (core, 1 - core):
             send(mine, mine, 2, nrm_sem, place(m, c))
     send(mine, mine, 2, nrm_sem, partner)
-    for t in range(3):
-        early(t, 2, own.at[0])
+    early(2, own.at[0], 0, EARLY)
+    early(0, par, AHEAD, EARLY)
+    early(1, acc, AHEAD, EARLY)
     wait_rows(nrm_sem, groups - 1)
     square = jnp.sum(jnp.sum(slots[...], axis=0, keepdims=True), axis=1, keepdims=True)
     norm = jnp.sqrt(square)
@@ -178,26 +190,28 @@
         a_new = a + h * h
         return a_new, w - rate * h / (jnp.sqrt(a_new) + EPS)
 
-    for p in (*range(1, PIECES), 0):
-        for t in range(3):
-            start, size = pieces[t][p]
+    heads = [cut(s0 + EARLY, size - EARLY, 3) + [(s0, EARLY)] for s0, size in thirds]
+    for p in range(4):
+        for t in range(3):
+            start, size = heads[t][p]
             r = pl.ds(start, size)
             newa_ref[r], full[pl.ds(base(0, core) + start, size)] = update(par[r], acc[r], own[0, r])
-            if p:
+            if p < 3:
                 gather(0, t, 0, far_sem.at[0], start, size)
     for j in (1, 2):
         for t in range(3):
             gather(0, t, j, far_sem.at[j], *thirds[t])
     forward(0, 0, blk)
-    wait_rows(raw_sem, n_raw)
+    wait_rows(raw_sem, 9 * EARLY)
     for t in range(3):
-        start, size = pieces[t][0]
-        r = pl.ds(0, size)
-        full[pl.ds(base(ORDERS[t][2], core) + start, size)] = update(
+        r = pl.ds(0, EARLY)
+        full[pl.ds(base(ORDERS[t][2], core) + thirds[t][0], EARLY)] = update(
             raw[3 * t, r], raw[3 * t + 1, r], raw[3 * t + 2, r])[1]
 
+    tails = [cut(s0, size - BOTH, PIECES) for s0, size in thirds]
+    ends = [(s0 + size - BOTH, BOTH) for s0, size in thirds]
     for step in range(6):
-        wait_rows(far_sem.at[step], blk if step else blk - n_raw // 3)
+        wait_rows(far_sem.at[step], blk if step else blk - 3 * EARLY)
         for t in range(3):
             c, b, a = ORDERS[t]
             m = (a, b, c, a + b, a + c, b + c)[step]
@@ -207,18 +221,43 @@
                 gather(m, t, 2, far_sem.at[4 + step], *thirds[t])
             if step == 3:
                 for p in range(PIECES):
-                    r = rows(m, *pieces[t][p])
+                    r = rows(m, *tails[t][p])
                     send(r, r, 3, near_sem.at[p], place(ORDERS[t][0], 1 - core))
+        if step == 3:
+            last = [(rows(a + b, *ends[t]), c) for t, (c, b, a) in enumerate(ORDERS)]
+
+            @pl.when(core == 0)
+            def _():
+                for r, c in last:
+                    send(r, r, 3, nrm_sem, place(c, 0))
+
+            for r, c in last:
+                send(r, r, 3, near_sem.at[PIECES + 1], place(c, 1 - core))
         for t in range(3):
             c, b, a = ORDERS[t]
             forward((a, b, c, a + b, a + c, b + c)[step], *thirds[t])
     for p in range(PIECES):
-        wait_rows(near_sem.at[p], sum(pieces[t][p][1] for t in range(3)))
-        for t in range(3):
-            forward(all_bits, *pieces[t][p], 1 - core)
-    wait_rows(near_sem.at[PIECES], 8 * blk)
-
-    for kind, n in enumerate((8 * blk, 7 * blk, groups - 1, 7 * blk - n_raw // 3, 8 * blk, n_raw)):
+        wait_rows(near_sem.at[p], sum(tails[t][p][1] for t in range(3)))
+        for t in range(3):
+            forward(all_bits, *tails[t][p], 1 - core)
+    n_both = sum(size for _, size in ends)
+    wait_rows(near_sem.at[PIECES + 1], n_both)
+
+    @pl.when(core == 0)
+    def _():
+        for t in range(3):
+            forward(all_bits, *ends[t], 1)
+        wait_rows(nrm_sem, n_both)
+        wait_rows(near_sem.at[PIECES], 8 * blk - n_both)
+        wait_rows(send_sem.at[3], n_both)
+        wait_rows(send_sem.at[4], n_both)
+
+    @pl.when(core == 1)
+    def _():
+        wait_rows(near_sem.at[PIECES], 8 * blk)
+
+    for kind, n in enumerate(
+            (8 * blk - 3 * FIRST, 7 * blk + 3 * FIRST, groups - 1, 7 * blk - 3 * EARLY, 8 * blk - n_both, 9 * EARLY)):
         wait_rows(send_sem.at[kind], n)
 
 
@@ -274,10 +313,11 @@
                 pltpu.VMEM((8, pad, LANES), f32),
                 pltpu.VMEM((8, pad, LANES), f32),
                 pltpu.VMEM((21, third, LANES), f32),
+                pltpu.VMEM((3, FIRST, LANES), f32),
                 pltpu.VMEM((blk, LANES), f32),
                 pltpu.VMEM((blk, LANES), f32),
                 pltpu.VMEM((groups, LANES), f32),
-                pltpu.VMEM((9, third, LANES), f32),
+                pltpu.VMEM((9, EARLY, LANES), f32),
                 dma((5,)), dma((PIECES + 2,)), dma((7,)), dma, dma, dma((6,)),
             ],
             compiler_params=pltpu.CompilerParams(

time: 79.9 us -> 78.5 us (0.982)
  Pallas kernels: 77.9 us -> 76.4 us
    pallas_call x1, Pallas kernels: 75.2 us -> 73.7 us  [local_step(): pl.pallas_call(functools.partial(kernel, blk, third, groups), out_shape=(...]
where the time goes in v6:
time: 78.5 us; the launch traced here: 78.4 us
  Pallas kernels  76.4 us (97%)
  between operations  1.93 us (2%)
    pallas_call x1, Pallas kernels, local_step(): pl.pallas_call(functools.partial(kernel, blk, third, groups), out_shape=(...  73.7 us
    pallas_call x1, Pallas kernels, local_step(): pl.pallas_call(functools.partial(write_kernel, blk), out_shape=(jax.Shape...  2.69 us

profile of v6, /device:TPU:0, one launch (start us, length us, event | category | flops | bytes accessed | tf_op | source)
XLA Modules:
  0.0 78.4 jit_solution(9501148853327580541)
XLA Ops:
  1.9 73.7 %shard_map.84 = (f32[19536,128]{1,0:T(8,128)S(1)}, f32[1221,128]{1,0:T(8,128)S(1)}, f32[1,128]{1,0:T(1,128)S(1)}) custom-call(f32[]{:T(128)S(6)} %copy.9.rate_ref, f32[]{:T(128)S(6)} %copy.10.clip_ref, f32[19536,128]{1,0:T(8,128)} %bitcast.7, f32[1221,128]{1,0:T(8,128)} %bitcast.8, f32[1221,128]{1,0:T(8,128)} %bitcast.9), custom_call_target="tpu_custom_call" | custom-call | tf_op jit(solution)/shard_map/pallas_call | solution.py:303
  75.7 2.7 %shard_map.85 = (f32[1221,128]{1,0:T(8,128)}, f32[1221,128]{1,0:T(8,128)}, bf16[19536,128]{1,0:T(8,128)(2,1)}, f32[1,1]{1,0:T(1,128)}) custom-call(f32[19536,128]{1,0:T(8,128)S(1)} %get-tuple-element.11.full, f32[1221,128]{1,0:T(8,128)S(1)} %get-tuple-element.12.newa, f32[1,128]{1,0:T(1,128)S(1)} %get-tuple-element.13.norm), custom_call_target="tpu_custom_call" | custom-call | tf_op jit(solution)/shard_map/pallas_call | solution.py:327

commit v7 on v6

--- a/solution.py
+++ b/solution.py
@@ -28,7 +28,7 @@
     blk, third, groups,
     rate_ref, clip_ref, grad_hbm, par_hbm, acc_hbm,
     full, newa_ref, norm_ref,
-    own, part, recv, other, par, acc, slots, raw,
+    own, part, recv, guest, other, par, acc, slots, raw,
     load_sem, near_sem, far_sem, nrm_sem, raw_sem, send_sem,
 ):
     me = lax.axis_index("dp")
@@ -69,7 +69,7 @@
     acc_cp.start()
 
     barrier = pltpu.get_barrier_semaphore()
-    near = [place(d, c) for d in (X, Y, Z) for c in (core, 1 - core)] + [partner]
+    near = (partner, across[X], across[Y], across[Z])
     for dev in near:
         pl.semaphore_signal(barrier, inc=1, device_id=(dev,), device_id_type=MESH)
     pl.semaphore_wait(barrier, len(near))
@@ -83,9 +83,9 @@
 
     for t in range(3):
         s0, _ = thirds[t]
-        for c, dst in ((core, recv), (1 - core, other)):
+        for c, dst, i in ((core, recv, 0), (1 - core, guest, 7)):
             send(grad_hbm.at[pl.ds(base(all_bits, c) + s0, FIRST)], dst.at[t, pl.ds(0, FIRST)],
-                 1, far_sem.at[0], place(ORDERS[t][0], c))
+                 1, far_sem.at[i], across[ORDERS[t][0]])
     for p in range(PIECES):
         for t in range(3):
             exchange(all_bits, *pieces[t][p], p)
@@ -127,6 +127,8 @@
     for t in range(3):
         fold(unit(3, t) ^ ORDERS[t][0], *thirds[t])
         push(3, t, *thirds[t])
+    wait_rows(far_sem.at[7], 3 * FIRST)
+    send(guest, other, 0, near_sem.at[PIECES + 2], partner)
     for step in range(4):
         for t in range(3):
             fold(unit(step, t), *thirds[t])
@@ -140,7 +142,9 @@
     acc_cp.wait()
     total = jnp.zeros((1, LANES), jnp.float32)
     for step in range(7):
-        wait_rows(far_sem.at[step], blk if step else blk + 3 * FIRST)
+        wait_rows(far_sem.at[step], blk)
+        if step == 0:
+            wait_rows(near_sem.at[PIECES + 2], 3 * FIRST)
         for t in range(3):
             m = unit(step, t)
             s0, size = thirds[t]
@@ -257,7 +261,7 @@
         wait_rows(near_sem.at[PIECES], 8 * blk)
 
     for kind, n in enumerate(
-            (8 * blk - 3 * FIRST, 7 * blk + 3 * FIRST, groups - 1, 7 * blk - 3 * EARLY, 8 * blk - n_both, 9 * EARLY)):
+            (8 * blk, 7 * blk + 3 * FIRST, groups - 1, 7 * blk - 3 * EARLY, 8 * blk - n_both, 9 * EARLY)):
         wait_rows(send_sem.at[kind], n)
 
 
@@ -314,11 +318,12 @@
                 pltpu.VMEM((8, pad, LANES), f32),
                 pltpu.VMEM((21, third, LANES), f32),
                 pltpu.VMEM((3, FIRST, LANES), f32),
+                pltpu.VMEM((3, FIRST, LANES), f32),
                 pltpu.VMEM((blk, LANES), f32),
                 pltpu.VMEM((blk, LANES), f32),
                 pltpu.VMEM((groups, LANES), f32),
                 pltpu.VMEM((9, EARLY, LANES), f32),
-                dma((5,)), dma((PIECES + 2,)), dma((7,)), dma, dma, dma((6,)),
+                dma((5,)), dma((PIECES + 3,)), dma((8,)), dma, dma, dma((6,)),
             ],
             compiler_params=pltpu.CompilerParams(
                 collective_id=0, has_side_effects=True, vmem_limit_bytes=40 * 1024 * 1024),

time: 78.5 us -> 78.2 us (level)
  no operation moved by 1% of the time
where the time goes in v7:
time: 78.2 us; the launch traced here: 78.1 us
  Pallas kernels  76.2 us (97%)
  between operations  1.93 us (2%)
    pallas_call x1, Pallas kernels, local_step(): pl.pallas_call(functools.partial(kernel, blk, third, groups), out_shape=(...  73.5 us
    pallas_call x1, Pallas kernels, local_step(): pl.pallas_call(functools.partial(write_kernel, blk), out_shape=(jax.Shape...  2.69 us

profile of v7, /device:TPU:0, one launch (start us, length us, event | category | flops | bytes accessed | tf_op | source)
XLA Modules:
  0.0 78.1 jit_solution(5105262232450782543)
XLA Ops:
  1.9 73.5 %shard_map.84 = (f32[19536,128]{1,0:T(8,128)S(1)}, f32[1221,128]{1,0:T(8,128)S(1)}, f32[1,128]{1,0:T(1,128)S(1)}) custom-call(f32[]{:T(128)S(6)} %copy.9.rate_ref, f32[]{:T(128)S(6)} %copy.10.clip_ref, f32[19536,128]{1,0:T(8,128)} %bitcast.7, f32[1221,128]{1,0:T(8,128)} %bitcast.8, f32[1221,128]{1,0:T(8,128)} %bitcast.9), custom_call_target="tpu_custom_call" | custom-call | tf_op jit(solution)/shard_map/pallas_call | solution.py:307
  75.4 2.7 %shard_map.85 = (f32[1221,128]{1,0:T(8,128)}, f32[1221,128]{1,0:T(8,128)}, bf16[19536,128]{1,0:T(8,128)(2,1)}, f32[1,1]{1,0:T(1,128)}) custom-call(f32[19536,128]{1,0:T(8,128)S(1)} %get-tuple-element.11.full, f32[1221,128]{1,0:T(8,128)S(1)} %get-tuple-element.12.newa, f32[1,128]{1,0:T(1,128)S(1)} %get-tuple-element.13.norm), custom_call_target="tpu_custom_call" | custom-call | tf_op jit(solution)/shard_map/pallas_call | solution.py:332

commit v8 on v7

--- a/solution.py
+++ b/solution.py
@@ -15,7 +15,7 @@
 PIECES = 6
 AHEAD = 104
 EARLY = 160
-BOTH = 112
+BOTH = 120
 FIRST = 64
 
 
@@ -49,29 +49,28 @@
 
     thirds = [(third * t, min(third, blk - third * t)) for t in range(3)]
 
-    def send(src, dst, kind, rcv, dev):
+    def send(src, dst, rcv, dev):
         pltpu.make_async_remote_copy(
-            src_ref=src, dst_ref=dst, send_sem=send_sem.at[kind], recv_sem=rcv,
+            src_ref=src, dst_ref=dst, send_sem=send_sem, recv_sem=rcv,
             device_id=(dev,), device_id_type=MESH).start()
 
     def wait_rows(sem, n):
         ref = full.at[pl.ds(0, n)]
         pltpu.make_async_copy(ref, ref, sem).wait()
+
+    barrier = pltpu.get_barrier_semaphore()
+    near = (across[X], across[Y], across[Z], partner)
+    for dev in near:
+        pl.semaphore_signal(barrier, inc=1, device_id=(dev,), device_id_type=MESH)
 
     waves = ((X + Y + Z,), (X + Y, Y + Z, Z + X), (X, Y, Z, 0))
     for i, wave in enumerate(waves):
         for m in wave:
             pltpu.make_async_copy(
                 grad_hbm.at[pl.ds(base(m, core), blk)], own.at[m, pl.ds(0, blk)], load_sem.at[i]).start()
-    par_cp = pltpu.make_async_copy(par_hbm, par, load_sem.at[3])
-    par_cp.start()
-    acc_cp = pltpu.make_async_copy(acc_hbm, acc, load_sem.at[4])
-    acc_cp.start()
-
-    barrier = pltpu.get_barrier_semaphore()
-    near = (partner, across[X], across[Y], across[Z])
-    for dev in near:
-        pl.semaphore_signal(barrier, inc=1, device_id=(dev,), device_id_type=MESH)
+    pltpu.make_async_copy(par_hbm, par, load_sem.at[2]).start()
+    pltpu.make_async_copy(acc_hbm, acc, load_sem.at[2]).start()
+
     pl.semaphore_wait(barrier, len(near))
 
     all_bits = X + Y + Z
@@ -79,13 +78,13 @@
 
     def exchange(m, start, size, i):
         send(grad_hbm.at[pl.ds(base(m, 1 - core) + start, size)],
-             part.at[m, pl.ds(start, size)], 0, near_sem.at[i], partner)
+             part.at[m, pl.ds(start, size)], near_sem.at[i], partner)
 
     for t in range(3):
         s0, _ = thirds[t]
         for c, dst, i in ((core, recv, 0), (1 - core, guest, 7)):
             send(grad_hbm.at[pl.ds(base(all_bits, c) + s0, FIRST)], dst.at[t, pl.ds(0, FIRST)],
-                 1, far_sem.at[i], across[ORDERS[t][0]])
+                 far_sem.at[i], across[ORDERS[t][0]])
     for p in range(PIECES):
         for t in range(3):
             exchange(all_bits, *pieces[t][p], p)
@@ -107,7 +106,7 @@
         dim = ORDERS[t][PHASE[step]]
         s0 = thirds[t][0]
         send(own.at[unit(step, t) ^ dim, pl.ds(start, size)],
-             recv.at[3 * step + t, pl.ds(start - s0, size)], 1, far_sem.at[step], across[dim])
+             recv.at[3 * step + t, pl.ds(start - s0, size)], far_sem.at[step], across[dim])
 
     load_waits = [len(w) * blk for w in waves]
     wait_rows(load_sem.at[0], load_waits[0])
@@ -122,13 +121,13 @@
         for t in range(3):
             fold(unit(step, t) ^ ORDERS[t][0], *thirds[t])
             push(step, t, *thirds[t])
-    wait_rows(load_sem.at[2], load_waits[2])
+    wait_rows(load_sem.at[2], load_waits[2] + 2 * blk)
     wait_rows(near_sem.at[PIECES + 1], load_waits[2])
     for t in range(3):
         fold(unit(3, t) ^ ORDERS[t][0], *thirds[t])
         push(3, t, *thirds[t])
     wait_rows(far_sem.at[7], 3 * FIRST)
-    send(guest, other, 0, near_sem.at[PIECES + 2], partner)
+    send(guest, other, near_sem.at[PIECES + 2], partner)
     for step in range(4):
         for t in range(3):
             fold(unit(step, t), *thirds[t])
@@ -136,10 +135,8 @@
     def early(k, src, lo, hi):
         for t in range(3):
             send(src.at[pl.ds(thirds[t][0] + lo, hi - lo)], raw.at[3 * t + k, pl.ds(lo, hi - lo)],
-                 5, raw_sem, across[ORDERS[t][2]])
-
-    par_cp.wait()
-    acc_cp.wait()
+                 raw_sem, across[ORDERS[t][2]])
+
     total = jnp.zeros((1, LANES), jnp.float32)
     for step in range(7):
         wait_rows(far_sem.at[step], blk)
@@ -168,8 +165,8 @@
     mine = slots.at[pl.ds(me, 1)]
     for m in (7, 3, 6, 5, 1, 2, 4):
         for c in (core, 1 - core):
-            send(mine, mine, 2, nrm_sem, place(m, c))
-    send(mine, mine, 2, nrm_sem, partner)
+            send(mine, mine, nrm_sem, place(m, c))
+    send(mine, mine, nrm_sem, partner)
     early(2, own.at[0], 0, EARLY)
     early(0, par, AHEAD, EARLY)
     early(1, acc, AHEAD, EARLY)
@@ -184,10 +181,10 @@
         return full.at[pl.ds(base(m, c) + start, size)]
 
     def gather(m, t, j, rcv, start, size):
-        send(rows(m, start, size), rows(m, start, size), 3, rcv, across[ORDERS[t][2 - j]])
+        send(rows(m, start, size), rows(m, start, size), rcv, across[ORDERS[t][2 - j]])
 
     def forward(m, start, size, c=core):
-        send(rows(m, start, size, c), rows(m, start, size, c), 4, near_sem.at[PIECES], partner)
+        send(rows(m, start, size, c), rows(m, start, size, c), near_sem.at[PIECES], partner)
 
     def update(w, a, total):
         h = total * (1.0 / groups) * scale
@@ -226,17 +223,17 @@
             if step == 3:
                 for p in range(PIECES):
                     r = rows(m, *tails[t][p])
-                    send(r, r, 3, near_sem.at[p], place(ORDERS[t][0], 1 - core))
+                    send(r, r, near_sem.at[p], place(ORDERS[t][0], 1 - core))
         if step == 3:
             last = [(rows(a + b, *ends[t]), c) for t, (c, b, a) in enumerate(ORDERS)]
 
             @pl.when(core == 0)
             def _():
                 for r, c in last:
-                    send(r, r, 3, nrm_sem, place(c, 0))
+                    send(r, r, nrm_sem, place(c, 0))
 
             for r, c in last:
-                send(r, r, 3, near_sem.at[PIECES + 1], place(c, 1 - core))
+                send(r, r, near_sem.at[PIECES + 1], place(c, 1 - core))
         for t in range(3):
             c, b, a = ORDERS[t]
             forward((a, b, c, a + b, a + c, b + c)[step], *thirds[t])
@@ -253,16 +250,14 @@
             forward(all_bits, *ends[t], 1)
         wait_rows(nrm_sem, n_both)
         wait_rows(near_sem.at[PIECES], 8 * blk - n_both)
-        wait_rows(send_sem.at[3], n_both)
-        wait_rows(send_sem.at[4], n_both)
+        wait_rows(send_sem, 2 * n_both)
 
     @pl.when(core == 1)
     def _():
         wait_rows(near_sem.at[PIECES], 8 * blk)
 
-    for kind, n in enumerate(
-            (8 * blk, 7 * blk + 3 * FIRST, groups - 1, 7 * blk - 3 * EARLY, 8 * blk - n_both, 9 * EARLY)):
-        wait_rows(send_sem.at[kind], n)
+    for n in (8 * blk, 7 * blk + 3 * FIRST, groups - 1, 7 * blk - 3 * EARLY, 8 * blk - n_both, 9 * EARLY):
+        wait_rows(send_sem, n)
 
 
 def write_kernel(blk, full, newa, norm, newp_hbm, newa_hbm, copy_hbm, norm_hbm, buf, one, sems):
@@ -323,7 +318,7 @@
                 pltpu.VMEM((blk, LANES), f32),
                 pltpu.VMEM((groups, LANES), f32),
                 pltpu.VMEM((9, EARLY, LANES), f32),
-                dma((5,)), dma((PIECES + 3,)), dma((8,)), dma, dma, dma((6,)),
+                dma((3,)), dma((PIECES + 3,)), dma((8,)), dma, dma, dma,
             ],
             compiler_params=pltpu.CompilerParams(
                 collective_id=0, has_side_effects=True, vmem_limit_bytes=40 * 1024 * 1024),

time: 78.2 us -> 78.1 us (level)
  no operation moved by 1% of the time
where the time goes in v8:
time: 78.1 us; the launch traced here: 78 us
  Pallas kernels  76.1 us (97%)
  between operations  1.93 us (2%)
    pallas_call x1, Pallas kernels, local_step(): pl.pallas_call(functools.partial(kernel, blk, third, groups), out_shape=(...  73.4 us
    pallas_call x1, Pallas kernels, local_step(): pl.pallas_call(functools.partial(write_kernel, blk), out_shape=(jax.Shape...  2.69 us

profile of v8, /device:TPU:0, one launch (start us, length us, event | category | flops | bytes accessed | tf_op | source)
XLA Modules:
  0.0 78.0 jit_solution(623698639340353292)
XLA Ops:
  1.9 73.4 %shard_map.84 = (f32[19536,128]{1,0:T(8,128)S(1)}, f32[1221,128]{1,0:T(8,128)S(1)}, f32[1,128]{1,0:T(1,128)S(1)}) custom-call(f32[]{:T(128)S(6)} %copy.9.rate_ref, f32[]{:T(128)S(6)} %copy.10.clip_ref, f32[19536,128]{1,0:T(8,128)} %bitcast.7, f32[1221,128]{1,0:T(8,128)} %bitcast.8, f32[1221,128]{1,0:T(8,128)} %bitcast.9), custom_call_target="tpu_custom_call" | custom-call | tf_op jit(solution)/shard_map/pallas_call | solution.py:302
  75.3 2.7 %shard_map.85 = (f32[1221,128]{1,0:T(8,128)}, f32[1221,128]{1,0:T(8,128)}, bf16[19536,128]{1,0:T(8,128)(2,1)}, f32[1,1]{1,0:T(1,128)}) custom-call(f32[19536,128]{1,0:T(8,128)S(1)} %get-tuple-element.11.full, f32[1221,128]{1,0:T(8,128)S(1)} %get-tuple-element.12.newa, f32[1,128]{1,0:T(1,128)S(1)} %get-tuple-element.13.norm), custom_call_target="tpu_custom_call" | custom-call | tf_op jit(solution)/shard_map/pallas_call | solution.py:327

commit v9 on v8

--- a/solution.py
+++ b/solution.py
@@ -11,7 +11,7 @@
 X, Y, Z = 1, 2, 4
 ORDERS = ((X, Y, Z), (Y, Z, X), (Z, X, Y))
 MESH = pl.DeviceIdType.MESH
-TILES = 12
+TILES = 20
 PIECES = 6
 AHEAD = 104
 EARLY = 160
@@ -164,7 +164,7 @@
     slots[pl.ds(me, 1)] = total
     mine = slots.at[pl.ds(me, 1)]
     for m in (7, 3, 6, 5, 1, 2, 4):
-        for c in (core, 1 - core):
+        for c in (1 - core, core):
             send(mine, mine, nrm_sem, place(m, c))
     send(mine, mine, nrm_sem, partner)
     early(2, own.at[0], 0, EARLY)
@@ -191,13 +191,13 @@
         a_new = a + h * h
         return a_new, w - rate * h / (jnp.sqrt(a_new) + EPS)
 
-    heads = [cut(s0 + EARLY, size - EARLY, 3) + [(s0, EARLY)] for s0, size in thirds]
-    for p in range(4):
+    heads = [cut(s0 + EARLY, size - EARLY, 4) + [(s0, EARLY)] for s0, size in thirds]
+    for p in range(5):
         for t in range(3):
             start, size = heads[t][p]
             r = pl.ds(start, size)
             newa_ref[r], full[pl.ds(base(0, core) + start, size)] = update(par[r], acc[r], own[0, r])
-            if p < 3:
+            if p < 4:
                 gather(0, t, 0, far_sem.at[0], start, size)
     for j in (1, 2):
         for t in range(3):

time: 78.1 us -> 78.1 us (level)
  no operation moved by 1% of the time
where the time goes in v9:
time: 78.1 us; the launch traced here: 77.9 us
  Pallas kernels  76 us (97%)
  between operations  1.93 us (2%)
    pallas_call x1, Pallas kernels, local_step(): pl.pallas_call(functools.partial(kernel, blk, third, groups), out_shape=(...  73.3 us
    pallas_call x1, Pallas kernels, local_step(): pl.pallas_call(functools.partial(write_kernel, blk), out_shape=(jax.Shape...  2.67 us

profile of v9, /device:TPU:0, one launch (start us, length us, event | category | flops | bytes accessed | tf_op | source)
XLA Modules:
  0.0 77.9 jit_solution(11616740546414594724)
XLA Ops:
  1.9 73.3 %shard_map.84 = (f32[19536,128]{1,0:T(8,128)S(1)}, f32[1221,128]{1,0:T(8,128)S(1)}, f32[1,128]{1,0:T(1,128)S(1)}) custom-call(f32[]{:T(128)S(6)} %copy.9.rate_ref, f32[]{:T(128)S(6)} %copy.10.clip_ref, f32[19536,128]{1,0:T(8,128)} %bitcast.7, f32[1221,128]{1,0:T(8,128)} %bitcast.8, f32[1221,128]{1,0:T(8,128)} %bitcast.9), custom_call_target="tpu_custom_call" | custom-call | tf_op jit(solution)/shard_map/pallas_call | solution.py:302
  75.3 2.7 %shard_map.85 = (f32[1221,128]{1,0:T(8,128)}, f32[1221,128]{1,0:T(8,128)}, bf16[19536,128]{1,0:T(8,128)(2,1)}, f32[1,1]{1,0:T(1,128)}) custom-call(f32[19536,128]{1,0:T(8,128)S(1)} %get-tuple-element.11.full, f32[1221,128]{1,0:T(8,128)S(1)} %get-tuple-element.12.newa, f32[1,128]{1,0:T(1,128)S(1)} %get-tuple-element.13.norm), custom_call_target="tpu_custom_call" | custom-call | tf_op jit(solution)/shard_map/pallas_call | solution.py:327

commit v10 on v9

--- a/solution.py
+++ b/solution.py
@@ -13,9 +13,9 @@
 MESH = pl.DeviceIdType.MESH
 TILES = 20
 PIECES = 6
-AHEAD = 104
+AHEAD = 106
 EARLY = 160
-BOTH = 120
+BOTH = 112
 FIRST = 64
 
 

time: 78.1 us -> 78.1 us (level)
  no operation moved by 1% of the time
where the time goes in v10:
time: 78.1 us; the launch traced here: 78 us
  Pallas kernels  76 us (97%)
  between operations  1.93 us (2%)
    pallas_call x1, Pallas kernels, local_step(): pl.pallas_call(functools.partial(kernel, blk, third, groups), out_shape=(...  73.4 us
    pallas_call x1, Pallas kernels, local_step(): pl.pallas_call(functools.partial(write_kernel, blk), out_shape=(jax.Shape...  2.67 us

profile of v10, /device:TPU:0, one launch (start us, length us, event | category | flops | bytes accessed | tf_op | source)
XLA Modules:
  0.0 78.0 jit_solution(10348083676437501638)
XLA Ops:
  1.9 73.4 %shard_map.84 = (f32[19536,128]{1,0:T(8,128)S(1)}, f32[1221,128]{1,0:T(8,128)S(1)}, f32[1,128]{1,0:T(1,128)S(1)}) custom-call(f32[]{:T(128)S(6)} %copy.9.rate_ref, f32[]{:T(128)S(6)} %copy.10.clip_ref, f32[19536,128]{1,0:T(8,128)} %bitcast.7, f32[1221,128]{1,0:T(8,128)} %bitcast.8, f32[1221,128]{1,0:T(8,128)} %bitcast.9), custom_call_target="tpu_custom_call" | custom-call | tf_op jit(solution)/shard_map/pallas_call | solution.py:302
  75.3 2.7 %shard_map.85 = (f32[1221,128]{1,0:T(8,128)}, f32[1221,128]{1,0:T(8,128)}, bf16[19536,128]{1,0:T(8,128)(2,1)}, f32[1,1]{1,0:T(1,128)}) custom-call(f32[19536,128]{1,0:T(8,128)S(1)} %get-tuple-element.11.full, f32[1221,128]{1,0:T(8,128)S(1)} %get-tuple-element.12.newa, f32[1,128]{1,0:T(1,128)S(1)} %get-tuple-element.13.norm), custom_call_target="tpu_custom_call" | custom-call | tf_op jit(solution)/shard_map/pallas_call | solution.py:327

commit v11 on v10

--- a/solution.py
+++ b/solution.py
@@ -13,7 +13,7 @@
 MESH = pl.DeviceIdType.MESH
 TILES = 20
 PIECES = 6
-AHEAD = 106
+AHEAD = 104
 EARLY = 160
 BOTH = 112
 FIRST = 64

time: 78.1 us -> 78.1 us (level)
  no operation moved by 1% of the time
where the time goes in v11:
time: 78.1 us; the launch traced here: 77.9 us
  Pallas kernels  76 us (97%)
  between operations  1.93 us (2%)
    pallas_call x1, Pallas kernels, local_step(): pl.pallas_call(functools.partial(kernel, blk, third, groups), out_shape=(...  73.3 us
    pallas_call x1, Pallas kernels, local_step(): pl.pallas_call(functools.partial(write_kernel, blk), out_shape=(jax.Shape...  2.67 us

profile of v11, /device:TPU:0, one launch (start us, length us, event | category | flops | bytes accessed | tf_op | source)
XLA Modules:
  0.0 77.9 jit_solution(3459414360955331054)
XLA Ops:
  1.9 73.3 %shard_map.84 = (f32[19536,128]{1,0:T(8,128)S(1)}, f32[1221,128]{1,0:T(8,128)S(1)}, f32[1,128]{1,0:T(1,128)S(1)}) custom-call(f32[]{:T(128)S(6)} %copy.9.rate_ref, f32[]{:T(128)S(6)} %copy.10.clip_ref, f32[19536,128]{1,0:T(8,128)} %bitcast.7, f32[1221,128]{1,0:T(8,128)} %bitcast.8, f32[1221,128]{1,0:T(8,128)} %bitcast.9), custom_call_target="tpu_custom_call" | custom-call | tf_op jit(solution)/shard_map/pallas_call | solution.py:302
  75.3 2.7 %shard_map.85 = (f32[1221,128]{1,0:T(8,128)}, f32[1221,128]{1,0:T(8,128)}, bf16[19536,128]{1,0:T(8,128)(2,1)}, f32[1,1]{1,0:T(1,128)}) custom-call(f32[19536,128]{1,0:T(8,128)S(1)} %get-tuple-element.11.full, f32[1221,128]{1,0:T(8,128)S(1)} %get-tuple-element.12.newa, f32[1,128]{1,0:T(1,128)S(1)} %get-tuple-element.13.norm), custom_call_target="tpu_custom_call" | custom-call | tf_op jit(solution)/shard_map/pallas_call | solution.py:327
